TPU v7x, 512 devices: a whole 4x8x8 slice. The times are simulated.
512 devices in a mesh: enc: 16 (over y, x_lo), slab: 32 (over x_hi, z, core).
Axes of the slice: x: 4 (x_hi: 2, x_lo: 2; x = x_hi * 2 + x_lo), y: 8, z: 8, core: 2. Of those that a mesh axis runs over, the one named last changes fastest.
Arguments:
- tokens: bfloat16 [32768, 1024], P(('slab', 'enc')), may hold values from -6 to 6
- cotangent: bfloat16 [32768, 1024], P(('slab', 'enc')), may hold values from -6 to 6
- w_qkv: bfloat16 [1024, 3072], P('slab', 'enc'), may hold values from -0.5 to 0.5
- w_out: bfloat16 [1024, 1024], P('enc', 'slab'), may hold values from -0.1875 to 0.1875
- mod_scale: float32 [1024], replicated, may hold values from -0.5 to 0.5
- mod_shift: float32 [1024], replicated, may hold values from -0.5 to 0.5
- mod_gate: float32 [1024], replicated, may hold values from 0.5 to 1.5
- counts: int32 [64], P('slab'), may hold values from 64 to 512
- edge_index: int32 [64, 128], P('slab'), may hold values from 0 to 1023
Outputs:
- grad_tokens: bfloat16 [32768, 1024], P(('slab', 'enc'))
- grad_qkv: float32 [1024, 3072], P('slab', 'enc')
- grad_out: float32 [1024, 1024], P('enc', 'slab')
Inputs may be any that keep to these rules, and one draw needn't show every extreme that they name: The first counts[w] slots of window w hold voxels; the rest are padding. `edge_index`: A row index within the preceding slab's 2 * 512 rows.
All inputs are finite; a program needn't handle non-finite values.
Results may differ from a plain program's by a relative error of at most 0.023.
Values may be sent and summed in bfloat16 or wider, within the bound.
A program may use at most 64 MiB of HBM per device.

v0:
```python
import jax
import jax.numpy as jnp
from jax import lax
from jax.sharding import PartitionSpec as P

HD = 64
EPS = 1e-06


def in_one_piece(arrays, axis, dim, along):
    widths = [a.shape[along] for a in arrays]
    both = jnp.concatenate(arrays, axis=along)
    whole = lax.all_gather(both, axis, axis=dim, tiled=True)
    return tuple(jnp.split(whole, [sum(widths[:k]) for k in range(1, len(widths))], axis=along))


def turned_gather(arrays, axis, dims):
    turned = [jnp.moveaxis(a, dim, 0) for a, dim in zip(arrays, dims)]
    widths = [t[0].size for t in turned]
    both = jnp.concatenate([t.reshape(-1, w) for t, w in zip(turned, widths)], axis=1)
    whole = lax.all_gather(both, axis, axis=0, tiled=True)
    blocks = jnp.split(whole, [sum(widths[:k]) for k in range(1, len(widths))], axis=1)
    return tuple(
        (
            jnp.moveaxis(b.reshape(-1, *t.shape[1:]), 0, dim)
            for b, t, dim in zip(blocks, turned, dims)
        )
    )


def shifted(block, axis, distance):
    devices = range(lax.axis_size(axis))
    route = [(i - distance, i) for i in devices if i - distance in devices]
    return lax.ppermute(block, axis, route)


def in_blocks(array, dim, peers):
    before, after = (array.shape[:dim], array.shape[dim + 1 :])
    return jnp.moveaxis(array.reshape(*before, peers, -1, *after), dim, 0)


def sum_at_owner(array, axis, dim):
    blocks = in_blocks(array, dim, lax.axis_size(axis))
    arrived = lax.all_to_all(blocks, axis, split_axis=0, concat_axis=0, tiled=True)
    return arrived.astype(jnp.float32).sum(axis=0)


def statistics(features):
    widened = features.astype(jnp.float32)
    average = jnp.mean(widened, 1, keepdims=True)
    centred = widened - average
    variance = jnp.mean(centred * centred, 1, keepdims=True)
    inv_std = lax.rsqrt(variance + EPS)
    return (centred * inv_std, inv_std)


def attend(query, key_vals, edge_vals, counts, edge_live, upstream, out_rows):
    windows = counts.shape[0]
    row_count = query.shape[0]
    win_size = row_count // windows
    head_size = query.shape[1]
    factor = head_size ** (-0.5)
    query_win = query.reshape(windows, win_size, head_size)
    keys_all = jnp.concatenate([key_vals.reshape(windows, win_size, 2 * head_size), edge_vals], 1)
    key_part = keys_all[:, :, :head_size]
    value_part = keys_all[:, :, head_size:]
    position = jnp.arange(win_size, dtype=jnp.int32)
    own_live = position[None, :] < counts[:, None]
    key_live = jnp.concatenate(
        [own_live, jnp.broadcast_to(edge_live[:, None], (windows, edge_vals.shape[1]))], 1
    )
    row_live = own_live.astype(jnp.float32)[:, :, None]
    scores = (
        jnp.einsum("wqd,wkd->wqk", query_win, key_part, preferred_element_type=jnp.float32) * factor
    )
    scores = jnp.where(key_live[:, None, :], scores, -1000000000.0)
    largest = jnp.max(scores, -1, keepdims=True)
    exponent = jnp.exp(scores - largest)
    softmax_p = exponent / jnp.sum(exponent, -1, keepdims=True)
    weights_b = softmax_p.astype(jnp.bfloat16)
    attended = (
        jnp.einsum("wqk,wkd->wqd", weights_b, value_part, preferred_element_type=jnp.float32)
        * row_live
    )
    attended = attended.astype(jnp.bfloat16).reshape(row_count, head_size)
    grad_att = jnp.dot(upstream, out_rows.T, preferred_element_type=jnp.float32).reshape(
        windows, win_size, head_size
    )
    grad_att = (grad_att * row_live).astype(jnp.bfloat16)
    grad_prob = jnp.einsum("wqd,wkd->wqk", grad_att, value_part, preferred_element_type=jnp.float32)
    grad_value = jnp.einsum("wqk,wqd->wkd", weights_b, grad_att, preferred_element_type=jnp.float32)
    grad_score = (
        softmax_p * (grad_prob - jnp.sum(grad_prob * softmax_p, -1, keepdims=True)) * factor
    )
    grad_score = grad_score.astype(jnp.bfloat16)
    grad_query = jnp.einsum(
        "wqk,wkd->wqd", grad_score, key_part, preferred_element_type=jnp.float32
    )
    grad_key = jnp.einsum("wqk,wqd->wkd", grad_score, query_win, preferred_element_type=jnp.float32)
    grad_pair = jnp.concatenate([grad_key, grad_value], -1)
    own_pair = grad_pair[:, :win_size].reshape(row_count, 2 * head_size)
    return (attended, grad_query.reshape(row_count, head_size), own_pair, grad_pair[:, win_size:])


def on_device(tokens, cotangent, w_qkv, w_out, mod_scale, mod_shift, mod_gate, counts, edge_index):
    features, upstream_in = in_one_piece((tokens, cotangent), "enc", 0, 1)
    weight_in, weight_out = turned_gather((w_qkv, w_out), "slab", (0, 1))
    normal_x, inv_std = statistics(features)
    gain = 1.0 + mod_scale
    normed = (normal_x * gain + mod_shift).astype(jnp.bfloat16)
    upstream = (upstream_in.astype(jnp.float32) * mod_gate).astype(jnp.bfloat16)
    windows = counts.shape[0]
    edge_count = edge_index.shape[1]
    heads_here = weight_out.shape[0] // HD
    pair_width = 2 * HD
    projected = jnp.dot(normed, weight_in, preferred_element_type=jnp.float32).astype(jnp.bfloat16)
    key_vals = projected[:, HD : 3 * HD]
    slab_index = lax.axis_index("slab")
    edge_live = jnp.full((windows,), slab_index > 0)
    flat_index = edge_index.reshape(-1)
    next_index = shifted(flat_index, "slab", -1)
    picked = jnp.take(key_vals, next_index, axis=0)
    edge_vals = shifted(picked, "slab", 1)
    edge_vals = edge_vals.reshape(windows, edge_count, heads_here * pair_width)
    attended, grad_query, own_pair, edge_pair = attend(
        projected[:, :HD], projected[:, HD:], edge_vals, counts, edge_live, upstream, weight_out
    )
    own_grads = own_pair
    edge_grads = edge_pair.reshape(-1, heads_here * pair_width)
    returned = shifted(edge_grads.astype(jnp.bfloat16), "slab", -1).astype(edge_grads.dtype)
    own_grads = own_grads.at[next_index].add(returned)
    grad_proj = jnp.concatenate([grad_query, own_grads], 1).astype(jnp.bfloat16)
    grad_q_local = jnp.dot(normed.T, grad_proj, preferred_element_type=jnp.float32)
    grad_o_local = jnp.dot(attended.T, upstream, preferred_element_type=jnp.float32)
    partial_value = jnp.dot(grad_proj, weight_in.T, preferred_element_type=jnp.float32)
    own_rows = tokens.shape[0]
    row_start = lax.axis_index("enc") * own_rows
    normal_own = lax.dynamic_slice_in_dim(normal_x, row_start, own_rows, 0)
    inv_own = lax.dynamic_slice_in_dim(inv_std, row_start, own_rows, 0)
    mine = sum_at_owner(partial_value.astype(jnp.bfloat16), "enc", 0)
    grad_hat = mine * gain
    grad_tokens = cotangent.astype(jnp.float32) + inv_own * (
        grad_hat
        - jnp.mean(grad_hat, 1, keepdims=True)
        - normal_own * jnp.mean(grad_hat * normal_own, 1, keepdims=True)
    )
    grad_qkv, grad_out = (
        sum_at_owner(grad_q_local.astype(jnp.bfloat16), "slab", 0),
        sum_at_owner(grad_o_local.astype(jnp.bfloat16), "slab", 1),
    )
    return (grad_tokens.astype(jnp.bfloat16), grad_qkv, grad_out)


def solution(mesh):
    placed = (
        P(("slab", "enc"), None),
        P(("slab", "enc"), None),
        P("slab", "enc"),
        P("enc", "slab"),
        P(),
        P(),
        P(),
        P("slab"),
        P("slab", None),
    )
    return jax.shard_map(
        on_device,
        mesh=mesh,
        in_specs=placed,
        out_specs=(P(("slab", "enc"), None), P("slab", "enc"), P("enc", "slab")),
        check_vma=False,
    )
```

profile of v0, /device:TPU:64, one launch (start us, length us, event | category | flops | bytes accessed | tf_op | source)
XLA Modules:
  0.0 280.1 jit_solution(14782367953100508507)
XLA Ops:
  7.2 1.7 pad_maximum_fusion.3
  8.9 1.9 collective-permute-start
  10.8 0.8 pad_maximum_fusion.8
  11.7 0.7 broadcast_add_fusion
  12.3 44.6 %all_gather.7 = bf16[1024,256]{1,0:T(8,128)(2,1)S(1)} all-gather(bf16[32,256]{1,0:T(8,128)(2,1)S(1)} %pad_maximum_fusion.8), channel_id=1, replica_groups=mesh['enc'=16,'slab'=32] {'slab'}, dimensions={0}, use_global_device_ids=true | all-gather | bytes 540672 | tf_op jit(solution)/shard_map/all_gather | solution.py:21
  56.9 0.7 iota_compare_fusion
  57.6 0.6 concatenate.20
  58.3 57.7 %all-gather.2.cloned.1.call-done = bf16[1024,2048]{1,0:T(8,128)(2,1)} async-done(((bf16[64,2048]{1,0:T(8,128)(2,1)}), bf16[1024,2048]{1,0:T(8,128)(2,1)}) %all-gather.2.cloned.1.call-update) | async-done | bytes 4194320 | tf_op jit(solution)/shard_map/all_gather | solution.py:13
  116.0 2.1 convert_reduce_fusion
  118.1 2.3 fusion.4
  120.4 1.3 convolution_convert_fusion.2
  121.7 0.2 copy.17
  121.9 0.9 gather_fusion
  122.9 1.9 collective-permute-start.1
  124.8 3.1 %fusion.16 = f32[1024,64]{0,1:T(8,128)} fusion(bf16[1024,2048]{1,0:T(8,128)(2,1)} %all-gather.2.cloned.1.call-done, f32[1024]{0:T(1024)S(1)} %copy-done.6, bf16[1024,256]{1,0:T(8,128)(2,1)S(1)} %all_gather.7), kind=kOutput, calls=%fused_computation.22 | convolution fusion | flops 137363456 | bytes 2625536 | tf_op jit(solution)/shard_map/dot_general | solution.py:86
  127.9 0.7 slice.28
  128.6 0.7 copy.63
  129.5 1.5 fusion.54
  131.0 4.0 %fusion.89 = (f32[2,512]{1,0:T(2,128)}, f32[2,512,640]{2,1,0:T(8,128)}) fusion(pred[2,640]{1,0:T(4,128)(4,1)} %concatenate.20, bf16[8,2,8,512]{3,2,1,0:T(8,128)(2,1)} %bitcast.62, bf16[2,512,128]{1,2,0:T(8,128)(2,1)S(1)} %bitcast.58, bf16[2,128,128]{1,2,0:T(8,128)(2,1)S(1)} %copy.19), kind=kOutput, calls=%fused_computation.94 | convolution fusion | flops 86835840 | bytes 3085568 | tf_op jit(solution)/shard_map/sub | solution.py:78
  135.1 2.3 fusion.29
  137.4 3.1 %fusion.27 = bf16[2,8,8,512]{3,2,1,0:T(8,128)(2,1)} fusion(f32[2,512]{1,0:T(2,128)S(1)} %get-tuple-element.6, bf16[2,128,128]{1,2,0:T(8,128)(2,1)S(1)} %copy.19, bf16[2,512,128]{1,2,0:T(8,128)(2,1)} %bitcast.56, f32[2,512]{1,0:T(2,128)} %get-tuple-element.7, pred[2,640]{1,0:T(4,128)(4,1)} %concatenate.20, bf16[8,2,8,512]{3,2,1,0:T(8,128)(2,1)} %bitcast.64), kind=kOutput, calls=%fused_computation.35 | convolution fusion | flops 171837056 | bytes 928256 | tf_op jit(solution)/shard_map/wqk,wkd->wqd/dot_general | solution.py:82
  140.4 8.7 %fusion.23 = bf16[2,512,64]{1,2,0:T(8,128)(2,1)} fusion(f32[2,512,640]{2,1,0:T(8,128)S(1)} %fusion.54, bf16[2,512,128]{1,2,0:T(8,128)(2,1)} %bitcast.57, bf16[2,128,128]{1,2,0:T(8,128)(2,1)S(1)} %copy.19, f32[2,512,640]{2,1,0:T(8,128)} %get-tuple-element.8, f32[2,512]{1,0:T(2,128)} %get-tuple-element.7), kind=kOutput, calls=%fused_computation.33 | convolution fusion | flops 88868480 | bytes 10952704 | tf_op jit(solution)/shard_map/wqk,wkd->wqd/dot_general | solution.py:96
  149.1 8.9 %fusion.10 = f32[2,640,64]{1,2,0:T(8,128)} fusion(f32[2,512,640]{2,1,0:T(8,128)S(1)} %fusion.54, bf16[8,2,8,512]{3,2,1,0:T(8,128)(2,1)} %bitcast.65, f32[2,512,640]{2,1,0:T(8,128)} %get-tuple-element.8, f32[2,512]{1,0:T(2,128)} %get-tuple-element.7), kind=kOutput, calls=%fused_computation.18 | convolution fusion | flops 88475264 | bytes 5705728 | tf_op jit(solution)/shard_map/wqk,wqd->wkd/dot_general | solution.py:99
  157.9 1.0 copy.35
  158.9 0.9 fusion.46
  159.9 3.8 %collective-permute-start.2 = (bf16[256,128]{1,0:T(8,128)(2,1)S(1)}, bf16[256,128]{1,0:T(8,128)(2,1)S(1)}, u32[]{:S(2)}, u32[]{:S(2)}) collective-permute-start(bf16[256,128]{1,0:T(8,128)(2,1)S(1)} %bitcast.67), channel_id=1, source_target_pairs={{1,0},{2,1},{3,2},{4,3},{5,4},{6,5},{7,6},{8,7},{9,8},{10,9},{11,1... | collective-permute-start | bytes 196616 | tf_op jit(solution)/shard_map/ppermute | solution.py:34
  163.7 2.2 fusion.22
  166.0 0.2 copy.24
  166.2 0.2 copy.29
  166.4 0.9 reshape.141
  167.2 11.2 %all-to-all-start.2 = ((bf16[32,2,1024]{2,1,0:T(2,128)(2,1)}), bf16[32,2,1024]{2,1,0:T(2,128)(2,1)S(1)}, u32[]{:S(2)}, u32[]{:S(2)}) async-start(bf16[32,2,1024]{2,1,0:T(2,128)(2,1)} %reshape.141), calls=%async_computation.2 | async-start | bytes 262144 | tf_op jit(solution)/shard_map/all_to_all | solution.py:44
  178.4 0.2 copy.30
  178.6 2.3 scatter_custom_fusion
  181.0 2.9 %convolution_convert_fusion.1 = bf16[1024,192]{0,1:T(8,128)(2,1)S(1)} fusion(f32[1024]{0:T(1024)S(1)} %copy-done.9, f32[1024]{0:T(1024)S(1)} %broadcast_add_fusion, bf16[1024,128]{1,0:T(8,128)(2,1)S(1)} %convert.12, bf16[1024,64]{1,0:T(8,128)(2,1)S(1)} %bitcast.52, f32[1024]{0:T(1024)S(1)} %add_rsqrt_fusion, f32[1024]{0:T(1024)S(1)} %broadcast_multiply_fusion, ...), kind=kOutput, calls=%fused_computation.29 | convolution fusion | flops 409927680 | bytes 2899968 | tf_op jit(solution)/shard_map/dot_general | solution.py:133
  183.9 1.0 copy.27
  184.9 4.4 %all-to-all-done.2 = bf16[32,2,1024]{2,1,0:T(2,128)(2,1)S(1)} async-done(((bf16[32,2,1024]{2,1,0:T(2,128)(2,1)}), bf16[32,2,1024]{2,1,0:T(2,128)(2,1)S(1)}, u32[]{:S(2)}, u32[]{:S(2)}) %all-to-all-start.2) | async-done | bytes 131104 | tf_op jit(solution)/shard_map/all_to_all | solution.py:44
  189.2 5.5 %all-to-all-start.1 = ((bf16[32,32,192]{2,1,0:T(8,128)(2,1)}), bf16[32,32,192]{2,1,0:T(8,128)(2,1)S(1)}, u32[]{:S(2)}, u32[]{:S(2)}) async-start(bf16[32,32,192]{2,1,0:T(8,128)(2,1)} %bitcast.7), calls=%async_computation.1 | async-start | bytes 1048576 | tf_op jit(solution)/shard_map/all_to_all | solution.py:44
  194.7 2.2 convolution_convert_fusion
  196.8 17.1 %all-to-all-done.1 = bf16[32,32,192]{2,1,0:T(8,128)(2,1)S(1)} async-done(((bf16[32,32,192]{2,1,0:T(8,128)(2,1)}), bf16[32,32,192]{2,1,0:T(8,128)(2,1)S(1)}, u32[]{:S(2)}, u32[]{:S(2)}) %all-to-all-start.1) | async-done | bytes 393248 | tf_op jit(solution)/shard_map/all_to_all | solution.py:44
  213.9 6.6 %all-to-all-start = ((bf16[16,64,1024]{2,1,0:T(8,128)(2,1)}), bf16[16,64,1024]{2,1,0:T(8,128)(2,1)S(1)}, u32[]{:S(2)}, u32[]{:S(2)}) async-start(bf16[16,64,1024]{2,1,0:T(8,128)(2,1)} %bitcast.6), calls=%async_computation | async-start | bytes 4194304 | tf_op jit(solution)/shard_map/all_to_all | solution.py:44
  220.6 4.1 %fusion.2 = f32[1024,1024]{1,0:T(8,128)} fusion(f32[1024]{0:T(1024)S(1)} %add_rsqrt_fusion, f32[1024]{0:T(1024)S(1)} %broadcast_multiply_fusion, bf16[1024,2048]{1,0:T(8,128)(2,1)} %all-gather.2.cloned.1.call-done), kind=kLoop, calls=%fused_computation.6 | loop fusion | flops 3145728 | bytes 6299648 | tf_op jit(solution)/shard_map/mul | solution.py:54
  224.7 0.2 reshape.142
  224.9 0.7 convert_reduce_fusion.3
  225.6 0.7 convert_reduce_fusion.2
  226.3 43.7 %all-to-all-done = bf16[16,64,1024]{2,1,0:T(8,128)(2,1)S(1)} async-done(((bf16[16,64,1024]{2,1,0:T(8,128)(2,1)}), bf16[16,64,1024]{2,1,0:T(8,128)(2,1)S(1)}, u32[]{:S(2)}, u32[]{:S(2)}) %all-to-all-start) | async-done | bytes 2097184 | tf_op jit(solution)/shard_map/all_to_all | solution.py:44
  270.0 0.4 convert_reduce_fusion.1
  270.4 1.1 multiply_reduce_fusion.2
  271.5 1.7 add_convert_fusion.3
  (38 shorter events, 0.7 us)
Async XLA Ops:
  7.2 108.8 %all-gather.2.cloned.1.call-start = ((), (), s32[]{:S(2)}) async-start(), calls=%async_computation.3 | async-start | bytes 4456448 | tf_op jit(solution)/shard_map/all_gather | solution.py:13
  8.9 111.5 %copy-start.8 = (f32[1024]{0:T(1024)S(1)}, f32[1024]{0:T(1024)}, u32[]{:S(2)}) copy-start(f32[1024]{0:T(1024)} %param.14) | copy-start | bytes 12292
  8.9 49.3 %collective-permute-start = (s32[256]{0:T(256)}, s32[256]{0:T(256)S(1)}, u32[]{:S(2)}, u32[]{:S(2)}) collective-permute-start(s32[256]{0:T(256)} %bitcast.70), channel_id=1, source_target_pairs={{1,0},{2,1},{3,2},{4,3},{5,4},{6,5},{7,6},{8,7},{9,8},{10,9},{11,1... | collective-permute-start | bytes 3080 | tf_op jit(solution)/shard_map/ppermute | solution.py:34
  58.2 57.7 %copy-start.5 = (s32[256]{0:T(256)}, s32[256]{0:T(256)S(1)}, u32[]{:S(2)}) copy-start(s32[256]{0:T(256)S(1)} %compare_select_fusion) | copy-start | bytes 3076
  116.0 4.4 %copy-start = (bf16[1024,2048]{1,0:T(8,128)(2,1)S(1)}, bf16[1024,2048]{1,0:T(8,128)(2,1)}, u32[]{:S(2)}) copy-start(bf16[1024,2048]{1,0:T(8,128)(2,1)} %all-gather.2.cloned.1.call-done) | copy-start | bytes 12582916
  120.4 4.4 %copy-start.6 = (f32[1024]{0:T(1024)S(1)}, f32[1024]{0:T(1024)}, u32[]{:S(2)}) copy-start(f32[1024]{0:T(1024)} %param.15) | copy-start | bytes 12292
  122.9 6.5 %collective-permute-start.1 = (bf16[256,128]{1,0:T(8,128)(2,1)S(1)}, bf16[256,128]{1,0:T(8,128)(2,1)S(1)}, u32[]{:S(2)}, u32[]{:S(2)}) collective-permute-start(bf16[256,128]{1,0:T(8,128)(2,1)S(1)} %broadcast_select_fusion), channel_id=1, source_target_pairs={{0,1},{1,2},{2,3},{3,4},{4,5},{5,6},{6,7},{7,8},{8,9},{9,10},{10,1... | collective-permute-start | bytes 196616 | tf_op jit(solution)/shard_map/ppermute | solution.py:34
  129.3 1.7 copy-start.2
  149.1 14.7 %copy-start.7 = (f32[1024]{0:T(1024)S(1)}, f32[1024]{0:T(1024)}, u32[]{:S(2)}) copy-start(f32[1024]{0:T(1024)} %param.15) | copy-start | bytes 12292
  157.9 8.0 %copy-start.1 = (f32[2,640,64]{1,2,0:T(8,128)S(1)}, f32[2,640,64]{1,2,0:T(8,128)}, u32[]{:S(2)}) copy-start(f32[2,640,64]{1,2,0:T(8,128)} %fusion.10) | copy-start | bytes 983044
  159.9 18.7 %collective-permute-start.2 = (bf16[256,128]{1,0:T(8,128)(2,1)S(1)}, bf16[256,128]{1,0:T(8,128)(2,1)S(1)}, u32[]{:S(2)}, u32[]{:S(2)}) collective-permute-start(bf16[256,128]{1,0:T(8,128)(2,1)S(1)} %bitcast.67), channel_id=1, source_target_pairs={{1,0},{2,1},{3,2},{4,3},{5,4},{6,5},{7,6},{8,7},{9,8},{10,9},{11,1... | collective-permute-start | bytes 196616 | tf_op jit(solution)/shard_map/ppermute | solution.py:34
  163.7 14.7 %copy-start.4 = (bf16[2,512,64]{1,2,0:T(8,128)(2,1)S(1)}, bf16[2,512,64]{1,2,0:T(8,128)(2,1)}, u32[]{:S(2)}) copy-start(bf16[2,512,64]{1,2,0:T(8,128)(2,1)} %fusion.23) | copy-start | bytes 393220
  165.9 15.0 %copy-start.9 = (f32[1024]{0:T(1024)S(1)}, f32[1024]{0:T(1024)}, u32[]{:S(2)}) copy-start(f32[1024]{0:T(1024)} %param.14) | copy-start | bytes 12292
  167.2 22.0 %all-to-all-start.2 = ((bf16[32,2,1024]{2,1,0:T(2,128)(2,1)}), bf16[32,2,1024]{2,1,0:T(2,128)(2,1)S(1)}, u32[]{:S(2)}, u32[]{:S(2)}) async-start(bf16[32,2,1024]{2,1,0:T(2,128)(2,1)} %reshape.141), calls=%async_computation.2 | async-start | bytes 262144 | tf_op jit(solution)/shard_map/all_to_all | solution.py:44
  189.2 24.7 %all-to-all-start.1 = ((bf16[32,32,192]{2,1,0:T(8,128)(2,1)}), bf16[32,32,192]{2,1,0:T(8,128)(2,1)S(1)}, u32[]{:S(2)}, u32[]{:S(2)}) async-start(bf16[32,32,192]{2,1,0:T(8,128)(2,1)} %bitcast.7), calls=%async_computation.1 | async-start | bytes 1048576 | tf_op jit(solution)/shard_map/all_to_all | solution.py:44
  213.9 56.0 %all-to-all-start = ((bf16[16,64,1024]{2,1,0:T(8,128)(2,1)}), bf16[16,64,1024]{2,1,0:T(8,128)(2,1)S(1)}, u32[]{:S(2)}, u32[]{:S(2)}) async-start(bf16[16,64,1024]{2,1,0:T(8,128)(2,1)} %bitcast.6), calls=%async_computation | async-start | bytes 4194304 | tf_op jit(solution)/shard_map/all_to_all | solution.py:44
  224.7 46.8 %copy-start.3 = (bf16[64,1024]{1,0:T(8,128)(2,1)S(1)}, bf16[64,1024]{1,0:T(8,128)(2,1)}, u32[]{:S(2)}) copy-start(bf16[64,1024]{1,0:T(8,128)(2,1)} %param.10) | copy-start | bytes 393220
Sparse Core Ops, SparseCore 0:
  10.1 105.8 all-gather.1
where the time goes:
time: 281 us; the launch traced here: 280 us
  waiting for transfers between devices  123 us (44%)
  blocking collectives  44.6 us (16%)
  matrix products  40.1 us (14%)
  starting transfers between devices  30.9 us (11%)
  other arithmetic  20.3 us (7%)
  between operations  14.4 us (5%)
  local copies, waits for them, and re-layouts  6.96 us (2%)
    all_to_all x3, waiting for transfers between devices, sum_at_owner(): lax.all_to_all(blocks, axis, split_axis=0, concat_axis=0, tiled=True)  65.1 us
    all_gather x1, waiting for transfers between devices, in_one_piece(): whole = lax.all_gather(both, axis, axis=dim, tiled=True)  57.7 us
    all_gather x1, blocking collectives, turned_gather(): whole = lax.all_gather(both, axis, axis=0, tiled=True)  44.6 us
    all_to_all x3, starting transfers between devices, sum_at_owner(): lax.all_to_all(blocks, axis, split_axis=0, concat_axis=0, tiled=True)  23.2 us
    dot_general x1, matrix products, attend(): jnp.einsum('wqk,wqd->wkd', grad_score, query_win, preferred_element_type=...  8.88 us
    dot_general x1, matrix products, attend(): jnp.einsum('wqk,wkd->wqd', grad_score, key_part, preferred_element_type=j...  8.65 us
    ppermute x3, starting transfers between devices, shifted(): return lax.ppermute(block, axis, route)  7.67 us
  transfers between devices with their start and end apart: 7, of which 4 were waited for; matrix products, arithmetic and copies ran while one was open for 9% of the time, Pallas kernels for 0%

commit v1 on v0

--- a/solution.py
+++ b/solution.py
@@ -18,7 +18,15 @@
     turned = [jnp.moveaxis(a, dim, 0) for a, dim in zip(arrays, dims)]
     widths = [t[0].size for t in turned]
     both = jnp.concatenate([t.reshape(-1, w) for t, w in zip(turned, widths)], axis=1)
-    whole = lax.all_gather(both, axis, axis=0, tiled=True)
+    whole = jnp.concatenate(
+        lax.all_to_all(
+            jnp.stack([both for _ in range(lax.axis_size(axis))]),
+            axis_name=axis,
+            split_axis=0,
+            concat_axis=0,
+        ),
+        axis=0,
+    )
     blocks = jnp.split(whole, [sum(widths[:k]) for k in range(1, len(widths))], axis=1)
     return tuple(
         (

time: 281 us -> 286 us (1.018)
  blocking collectives: 44.6 us -> 0 us
  waiting for transfers between devices: 123 us -> 158 us
  starting transfers between devices: 30.9 us -> 43.4 us
    all_gather x1 -> x0, blocking collectives: 44.6 us -> none  [turned_gather(): whole = lax.all_gather(both, axis, axis=0, tiled=True)]
    all_gather x1, waiting for transfers between devices: 57.7 us -> 92.7 us  [in_one_piece(): whole = lax.all_gather(both, axis, axis=dim, tiled=True)]
    all_to_all x0 -> x1, starting transfers between devices: none -> 12.8 us  [turned_gather(): lax.all_to_all(jnp.stack([both for _ in range(lax.axis_size(axis))]), axi...]
  transfers between devices with their start and end apart: 7 -> 8, of which waited for: 4 -> 4; matrix products, arithmetic and copies ran while one was open for 9% -> 11% of each run, Pallas kernels for 0% -> 0%
where the time goes in v1:
time: 286 us; the launch traced here: 285 us
  waiting for transfers between devices  158 us (55%)
  starting transfers between devices  43.4 us (15%)
  matrix products  41.6 us (15%)
  other arithmetic  20.2 us (7%)
  between operations  14.4 us (5%)
  local copies, waits for them, and re-layouts  7.81 us (3%)
    all_gather x1, waiting for transfers between devices, in_one_piece(): whole = lax.all_gather(both, axis, axis=dim, tiled=True)  92.7 us
    all_to_all x3, waiting for transfers between devices, sum_at_owner(): lax.all_to_all(blocks, axis, split_axis=0, concat_axis=0, tiled=True)  65.1 us
    all_to_all x3, starting transfers between devices, sum_at_owner(): lax.all_to_all(blocks, axis, split_axis=0, concat_axis=0, tiled=True)  22.9 us
    all_to_all x1, starting transfers between devices, turned_gather(): lax.all_to_all(jnp.stack([both for _ in range(lax.axis_size(axis))]), axi...  12.8 us
    dot_general x1, matrix products, attend(): jnp.einsum('wqk,wqd->wkd', grad_score, query_win, preferred_element_type=...  8.88 us
    dot_general x1, matrix products, attend(): jnp.einsum('wqk,wkd->wqd', grad_score, key_part, preferred_element_type=j...  8.65 us
    ppermute x3, starting transfers between devices, shifted(): return lax.ppermute(block, axis, route)  7.67 us
  transfers between devices with their start and end apart: 8, of which 4 were waited for; matrix products, arithmetic and copies ran while one was open for 11% of the time, Pallas kernels for 0%

profile of v1, /device:TPU:64, one launch (start us, length us, event | category | flops | bytes accessed | tf_op | source)
XLA Modules:
  0.0 285.2 jit_solution(13491893945591762261)
XLA Ops:
  7.2 1.7 pad_maximum_fusion.3
  8.9 1.9 collective-permute-start
  10.9 0.8 pad_maximum_fusion.8
  11.7 0.9 stack.2
  12.5 12.8 %all-to-all-start = ((bf16[32,32,256]{2,1,0:T(8,128)(2,1)}), bf16[32,32,256]{2,1,0:T(8,128)(2,1)S(1)}, u32[]{:S(2)}, u32[]{:S(2)}) async-start(bf16[32,32,256]{2,1,0:T(8,128)(2,1)} %stack.2), calls=%async_computation | async-start | bytes 1048576 | tf_op jit(solution)/shard_map/all_to_all | solution.py:22
  25.4 0.7 broadcast_add_fusion
  26.0 0.7 iota_compare_fusion
  26.8 0.6 concatenate.20
  27.4 92.7 %all-gather.2.cloned.1.call-done = bf16[1024,2048]{1,0:T(8,128)(2,1)} async-done(((bf16[64,2048]{1,0:T(8,128)(2,1)}), bf16[1024,2048]{1,0:T(8,128)(2,1)}) %all-gather.2.cloned.1.call-update) | async-done | bytes 4194320 | tf_op jit(solution)/shard_map/all_gather | solution.py:13
  120.1 1.9 convert_reduce_fusion
  122.0 2.3 fusion.4
  124.3 2.8 convolution_convert_fusion.2
  127.2 0.2 copy.17
  127.4 0.9 gather_fusion
  128.4 1.9 collective-permute-start.1
  130.3 3.1 %fusion.16 = f32[1024,64]{0,1:T(8,128)} fusion(bf16[1024,2048]{1,0:T(8,128)(2,1)} %all-gather.2.cloned.1.call-done, f32[1024]{0:T(1024)S(1)} %copy-done.5, bf16[1024,256]{1,0:T(8,128)(2,1)S(1)} %bitcast.54), kind=kOutput, calls=%fused_computation.22 | convolution fusion | flops 137363456 | bytes 2625536 | tf_op jit(solution)/shard_map/dot_general | solution.py:94
  133.4 0.7 slice.28
  134.1 0.7 copy.63
  135.0 1.5 fusion.54
  136.5 4.0 %fusion.89 = (f32[2,512]{1,0:T(2,128)}, f32[2,512,640]{2,1,0:T(8,128)}) fusion(pred[2,640]{1,0:T(4,128)(4,1)} %concatenate.20, bf16[8,2,8,512]{3,2,1,0:T(8,128)(2,1)} %bitcast.66, bf16[2,512,128]{1,2,0:T(8,128)(2,1)S(1)} %bitcast.62, bf16[2,128,128]{1,2,0:T(8,128)(2,1)S(1)} %copy.19), kind=kOutput, calls=%fused_computation.94 | convolution fusion | flops 86835840 | bytes 3085568 | tf_op jit(solution)/shard_map/sub | solution.py:86
  140.6 2.3 fusion.29
  142.9 3.1 %fusion.27 = bf16[2,8,8,512]{3,2,1,0:T(8,128)(2,1)} fusion(f32[2,512]{1,0:T(2,128)S(1)} %get-tuple-element.6, bf16[2,128,128]{1,2,0:T(8,128)(2,1)S(1)} %copy.19, bf16[2,512,128]{1,2,0:T(8,128)(2,1)} %bitcast.60, f32[2,512]{1,0:T(2,128)} %get-tuple-element.7, pred[2,640]{1,0:T(4,128)(4,1)} %concatenate.20, bf16[8,2,8,512]{3,2,1,0:T(8,128)(2,1)} %bitcast.68), kind=kOutput, calls=%fused_computation.35 | convolution fusion | flops 171837056 | bytes 928256 | tf_op jit(solution)/shard_map/wqk,wkd->wqd/dot_general | solution.py:90
  145.9 8.7 %fusion.23 = bf16[2,512,64]{1,2,0:T(8,128)(2,1)} fusion(f32[2,512,640]{2,1,0:T(8,128)S(1)} %fusion.54, bf16[2,512,128]{1,2,0:T(8,128)(2,1)} %bitcast.61, bf16[2,128,128]{1,2,0:T(8,128)(2,1)S(1)} %copy.19, f32[2,512,640]{2,1,0:T(8,128)} %get-tuple-element.8, f32[2,512]{1,0:T(2,128)} %get-tuple-element.7), kind=kOutput, calls=%fused_computation.33 | convolution fusion | flops 88868480 | bytes 10952704 | tf_op jit(solution)/shard_map/wqk,wkd->wqd/dot_general | solution.py:104
  154.6 8.9 %fusion.10 = f32[2,640,64]{1,2,0:T(8,128)} fusion(f32[2,512,640]{2,1,0:T(8,128)S(1)} %fusion.54, bf16[8,2,8,512]{3,2,1,0:T(8,128)(2,1)} %bitcast.69, f32[2,512,640]{2,1,0:T(8,128)} %get-tuple-element.8, f32[2,512]{1,0:T(2,128)} %get-tuple-element.7), kind=kOutput, calls=%fused_computation.18 | convolution fusion | flops 88475264 | bytes 5705728 | tf_op jit(solution)/shard_map/wqk,wqd->wkd/dot_general | solution.py:107
  163.4 1.0 copy.35
  164.4 0.9 fusion.46
  165.4 3.8 %collective-permute-start.2 = (bf16[256,128]{1,0:T(8,128)(2,1)S(1)}, bf16[256,128]{1,0:T(8,128)(2,1)S(1)}, u32[]{:S(2)}, u32[]{:S(2)}) collective-permute-start(bf16[256,128]{1,0:T(8,128)(2,1)S(1)} %bitcast.71), channel_id=1, source_target_pairs={{1,0},{2,1},{3,2},{4,3},{5,4},{6,5},{7,6},{8,7},{9,8},{10,9},{11,1... | collective-permute-start | bytes 196616 | tf_op jit(solution)/shard_map/ppermute | solution.py:42
  169.2 2.2 fusion.22
  171.5 0.2 copy.24
  171.7 0.2 copy.29
  171.9 0.9 reshape.147
  172.7 11.5 %all-to-all-start.3 = ((bf16[32,2,1024]{2,1,0:T(2,128)(2,1)}), bf16[32,2,1024]{2,1,0:T(2,128)(2,1)S(1)}, u32[]{:S(2)}, u32[]{:S(2)}) async-start(bf16[32,2,1024]{2,1,0:T(2,128)(2,1)} %reshape.147), calls=%async_computation.3 | async-start | bytes 262144 | tf_op jit(solution)/shard_map/all_to_all | solution.py:52
  184.4 2.3 scatter_custom_fusion
  186.7 2.9 %convolution_convert_fusion.1 = bf16[1024,192]{0,1:T(8,128)(2,1)S(1)} fusion(f32[1024]{0:T(1024)S(1)} %copy-done.8, f32[1024]{0:T(1024)S(1)} %broadcast_add_fusion, bf16[1024,128]{1,0:T(8,128)(2,1)S(1)} %convert.12, bf16[1024,64]{1,0:T(8,128)(2,1)S(1)} %bitcast.56, f32[1024]{0:T(1024)S(1)} %add_rsqrt_fusion, f32[1024]{0:T(1024)S(1)} %broadcast_multiply_fusion, ...), kind=kOutput, calls=%fused_computation.29 | convolution fusion | flops 409927680 | bytes 2899968 | tf_op jit(solution)/shard_map/dot_general | solution.py:141
  189.6 1.0 copy.27
  190.6 4.4 %all-to-all-done.3 = bf16[32,2,1024]{2,1,0:T(2,128)(2,1)S(1)} async-done(((bf16[32,2,1024]{2,1,0:T(2,128)(2,1)}), bf16[32,2,1024]{2,1,0:T(2,128)(2,1)S(1)}, u32[]{:S(2)}, u32[]{:S(2)}) %all-to-all-start.3) | async-done | bytes 131104 | tf_op jit(solution)/shard_map/all_to_all | solution.py:52
  195.0 5.5 %all-to-all-start.2 = ((bf16[32,32,192]{2,1,0:T(8,128)(2,1)}), bf16[32,32,192]{2,1,0:T(8,128)(2,1)S(1)}, u32[]{:S(2)}, u32[]{:S(2)}) async-start(bf16[32,32,192]{2,1,0:T(8,128)(2,1)} %bitcast.8), calls=%async_computation.2 | async-start | bytes 1048576 | tf_op jit(solution)/shard_map/all_to_all | solution.py:52
  200.5 2.2 convolution_convert_fusion
  202.6 17.1 %all-to-all-done.2 = bf16[32,32,192]{2,1,0:T(8,128)(2,1)S(1)} async-done(((bf16[32,32,192]{2,1,0:T(8,128)(2,1)}), bf16[32,32,192]{2,1,0:T(8,128)(2,1)S(1)}, u32[]{:S(2)}, u32[]{:S(2)}) %all-to-all-start.2) | async-done | bytes 393248 | tf_op jit(solution)/shard_map/all_to_all | solution.py:52
  219.7 6.0 %all-to-all-start.1 = ((bf16[16,64,1024]{2,1,0:T(8,128)(2,1)}), bf16[16,64,1024]{2,1,0:T(8,128)(2,1)S(1)}, u32[]{:S(2)}, u32[]{:S(2)}) async-start(bf16[16,64,1024]{2,1,0:T(8,128)(2,1)} %bitcast.7), calls=%async_computation.1 | async-start | bytes 4194304 | tf_op jit(solution)/shard_map/all_to_all | solution.py:52
  225.8 4.1 %fusion.2 = f32[1024,1024]{1,0:T(8,128)} fusion(f32[1024]{0:T(1024)S(1)} %add_rsqrt_fusion, f32[1024]{0:T(1024)S(1)} %broadcast_multiply_fusion, bf16[1024,2048]{1,0:T(8,128)(2,1)} %all-gather.2.cloned.1.call-done), kind=kLoop, calls=%fused_computation.6 | loop fusion | flops 3145728 | bytes 6299648 | tf_op jit(solution)/shard_map/mul | solution.py:62
  229.8 0.2 reshape.148
  230.1 0.7 convert_reduce_fusion.3
  230.7 0.7 convert_reduce_fusion.2
  231.5 43.7 %all-to-all-done.1 = bf16[16,64,1024]{2,1,0:T(8,128)(2,1)S(1)} async-done(((bf16[16,64,1024]{2,1,0:T(8,128)(2,1)}), bf16[16,64,1024]{2,1,0:T(8,128)(2,1)S(1)}, u32[]{:S(2)}, u32[]{:S(2)}) %all-to-all-start.1) | async-done | bytes 2097184 | tf_op jit(solution)/shard_map/all_to_all | solution.py:52
  275.1 0.4 convert_reduce_fusion.1
  275.5 1.1 multiply_reduce_fusion.2
  276.6 1.7 add_convert_fusion.3
  (38 shorter events, 0.8 us)
Async XLA Ops:
  7.2 112.9 %all-gather.2.cloned.1.call-start = ((), (), s32[]{:S(2)}) async-start(), calls=%async_computation.4 | async-start | bytes 4456448 | tf_op jit(solution)/shard_map/all_gather | solution.py:13
  8.9 18.4 %collective-permute-start = (s32[256]{0:T(256)}, s32[256]{0:T(256)S(1)}, u32[]{:S(2)}, u32[]{:S(2)}) collective-permute-start(s32[256]{0:T(256)} %bitcast.74), channel_id=1, source_target_pairs={{1,0},{2,1},{3,2},{4,3},{5,4},{6,5},{7,6},{8,7},{9,8},{10,9},{11,1... | collective-permute-start | bytes 3080 | tf_op jit(solution)/shard_map/ppermute | solution.py:42
  12.5 111.8 %copy-start.7 = (f32[1024]{0:T(1024)S(1)}, f32[1024]{0:T(1024)}, u32[]{:S(2)}) copy-start(f32[1024]{0:T(1024)} %param.14) | copy-start | bytes 12292
  12.5 111.8 %all-to-all-start = ((bf16[32,32,256]{2,1,0:T(8,128)(2,1)}), bf16[32,32,256]{2,1,0:T(8,128)(2,1)S(1)}, u32[]{:S(2)}, u32[]{:S(2)}) async-start(bf16[32,32,256]{2,1,0:T(8,128)(2,1)} %stack.2), calls=%async_computation | async-start | bytes 1048576 | tf_op jit(solution)/shard_map/all_to_all | solution.py:22
  27.4 92.7 %copy-start.4 = (s32[256]{0:T(256)}, s32[256]{0:T(256)S(1)}, u32[]{:S(2)}) copy-start(s32[256]{0:T(256)S(1)} %compare_select_fusion) | copy-start | bytes 3076
  124.3 6.0 %copy-start.5 = (f32[1024]{0:T(1024)S(1)}, f32[1024]{0:T(1024)}, u32[]{:S(2)}) copy-start(f32[1024]{0:T(1024)} %param.15) | copy-start | bytes 12292
  128.4 6.5 %collective-permute-start.1 = (bf16[256,128]{1,0:T(8,128)(2,1)S(1)}, bf16[256,128]{1,0:T(8,128)(2,1)S(1)}, u32[]{:S(2)}, u32[]{:S(2)}) collective-permute-start(bf16[256,128]{1,0:T(8,128)(2,1)S(1)} %broadcast_select_fusion), channel_id=1, source_target_pairs={{0,1},{1,2},{2,3},{3,4},{4,5},{5,6},{6,7},{7,8},{8,9},{9,10},{10,1... | collective-permute-start | bytes 196616 | tf_op jit(solution)/shard_map/ppermute | solution.py:42
  134.8 1.7 copy-start.1
  154.6 14.7 %copy-start.6 = (f32[1024]{0:T(1024)S(1)}, f32[1024]{0:T(1024)}, u32[]{:S(2)}) copy-start(f32[1024]{0:T(1024)} %param.15) | copy-start | bytes 12292
  163.4 8.0 %copy-start = (f32[2,640,64]{1,2,0:T(8,128)S(1)}, f32[2,640,64]{1,2,0:T(8,128)}, u32[]{:S(2)}) copy-start(f32[2,640,64]{1,2,0:T(8,128)} %fusion.10) | copy-start | bytes 983044
  165.4 19.0 %collective-permute-start.2 = (bf16[256,128]{1,0:T(8,128)(2,1)S(1)}, bf16[256,128]{1,0:T(8,128)(2,1)S(1)}, u32[]{:S(2)}, u32[]{:S(2)}) collective-permute-start(bf16[256,128]{1,0:T(8,128)(2,1)S(1)} %bitcast.71), channel_id=1, source_target_pairs={{1,0},{2,1},{3,2},{4,3},{5,4},{6,5},{7,6},{8,7},{9,8},{10,9},{11,1... | collective-permute-start | bytes 196616 | tf_op jit(solution)/shard_map/ppermute | solution.py:42
  169.2 15.0 %copy-start.3 = (bf16[2,512,64]{1,2,0:T(8,128)(2,1)S(1)}, bf16[2,512,64]{1,2,0:T(8,128)(2,1)}, u32[]{:S(2)}) copy-start(bf16[2,512,64]{1,2,0:T(8,128)(2,1)} %fusion.23) | copy-start | bytes 393220
  171.4 15.3 %copy-start.8 = (f32[1024]{0:T(1024)S(1)}, f32[1024]{0:T(1024)}, u32[]{:S(2)}) copy-start(f32[1024]{0:T(1024)} %param.14) | copy-start | bytes 12292
  172.7 22.3 %all-to-all-start.3 = ((bf16[32,2,1024]{2,1,0:T(2,128)(2,1)}), bf16[32,2,1024]{2,1,0:T(2,128)(2,1)S(1)}, u32[]{:S(2)}, u32[]{:S(2)}) async-start(bf16[32,2,1024]{2,1,0:T(2,128)(2,1)} %reshape.147), calls=%async_computation.3 | async-start | bytes 262144 | tf_op jit(solution)/shard_map/all_to_all | solution.py:52
  195.0 24.7 %all-to-all-start.2 = ((bf16[32,32,192]{2,1,0:T(8,128)(2,1)}), bf16[32,32,192]{2,1,0:T(8,128)(2,1)S(1)}, u32[]{:S(2)}, u32[]{:S(2)}) async-start(bf16[32,32,192]{2,1,0:T(8,128)(2,1)} %bitcast.8), calls=%async_computation.2 | async-start | bytes 1048576 | tf_op jit(solution)/shard_map/all_to_all | solution.py:52
  219.7 55.4 %all-to-all-start.1 = ((bf16[16,64,1024]{2,1,0:T(8,128)(2,1)}), bf16[16,64,1024]{2,1,0:T(8,128)(2,1)S(1)}, u32[]{:S(2)}, u32[]{:S(2)}) async-start(bf16[16,64,1024]{2,1,0:T(8,128)(2,1)} %bitcast.7), calls=%async_computation.1 | async-start | bytes 4194304 | tf_op jit(solution)/shard_map/all_to_all | solution.py:52
  229.8 46.8 %copy-start.2 = (bf16[64,1024]{1,0:T(8,128)(2,1)S(1)}, bf16[64,1024]{1,0:T(8,128)(2,1)}, u32[]{:S(2)}) copy-start(bf16[64,1024]{1,0:T(8,128)(2,1)} %param.10) | copy-start | bytes 393220
Sparse Core Ops, SparseCore 0:
  10.1 109.9 all-gather.1
